TPU v7x, 32 devices: a whole 2x2x4 slice. The times are simulated.
32 devices in a mesh: frame: 4 (over z), row: 8 (over y, x, core).
Axes of the slice: x: 2, y: 2, z: 4, core: 2. Of those that a mesh axis runs over, the one named last changes fastest.
Arguments:
- fine: bfloat16 [8, 320, 32, 128], P('frame', None, 'row'), may hold values from -6 to 6
- coarse: bfloat16 [4, 64, 1280], P(None, 'row', 'frame'), may hold values from -6 to 6
- w_qkv: bfloat16 [3, 1280, 1280], P(None, None, 'frame'), may hold values from -0.15625 to 0.15625
- w_out: bfloat16 [1280, 1280], P('frame'), may hold values from -0.15625 to 0.15625
- w_up: bfloat16 [1280, 320], P('frame'), may hold values from -0.15625 to 0.15625
- gain_one: float32 [320], replicated, may hold values from 0.1 to 1.9
- conv_space: bfloat16 [3, 3, 320, 320], replicated, may hold values from -0.109375 to 0.109375
- gain_two: float32 [320], replicated, may hold values from 0.1 to 1.9
- conv_time: bfloat16 [3, 320, 320], replicated, may hold values from -0.1875 to 0.1875
Outputs:
- result: bfloat16 [8, 320, 32, 128], P('frame', None, 'row')
All inputs are finite; a program needn't handle non-finite values.
Results may differ from a plain program's by a relative error of at most 0.013.
Values may be sent and summed in bfloat16 or wider, within the bound.
A program may use at most 64 MiB of HBM per device.

v0:
```python
import functools
import math

import jax
import jax.numpy as jnp
from jax import lax
from jax.experimental import pallas as pl
from jax.experimental.pallas import tpu as pltpu
from jax.sharding import PartitionSpec as P

HD = 80
UPSAMPLE = 8
MESH = pl.DeviceIdType.MESH
BF = jnp.bfloat16
F32 = jnp.float32


def silu(a):
    half = 0.5 * a
    return half + half * jnp.tanh(half)


def dot(a, b):
    return jnp.dot(a, b, preferred_element_type=F32)


def dot_t(a, b):
    return lax.dot_general(a, b, (((0,), (0,)), ((), ())), preferred_element_type=F32)


def kernel(
    nf, nr, cf_count, p_dev,
    fine_ref, coarse_ref, w_qkv_ref, w_out_ref, w_up_ref, gain_one_ref, conv_s_ref, gain_two_ref, conv_t_ref,
    out_ref,
    wq, wo, wu, cs, ct, cst, ctt, fb, cg, rs_send, rs_recv, up_send, up_recv, ub_send, ub, x3, n2, gain_one, gain_two,
    load_sem, halo_send, halo_recv, g_send, g_recv, r_send, r_recv, u_send, u_recv, b_send, b_recv,
):
    f_dev, rows, chans, width = fine_ref.shape
    cells, c_dev = coarse_ref.shape
    frames_ext = f_dev + 2
    rows_ext = rows + 2
    group = (width // UPSAMPLE) // p_dev
    n_groups = nr // group
    heads = c_dev // HD
    me_f = lax.axis_index("frame")
    me_r = lax.axis_index("row")
    my_group = me_r // group
    k_me = me_r % group
    first = k_me == 0
    last = k_me == group - 1

    parts = {
        "space0": (conv_s_ref.at[0], cs.at[0]),
        "qkv": (w_qkv_ref, wq),
        "out": (w_out_ref, wo),
        "space1": (conv_s_ref.at[1], cs.at[1]),
        "up": (w_up_ref, wu),
        "space2": (conv_s_ref.at[2], cs.at[2]),
        "time": (conv_t_ref, ct),
        "fine": (fine_ref, fb.at[pl.ds(1, f_dev), pl.ds(1, rows)]),
    }
    loads = {
        name: pltpu.make_async_copy(src, dst, load_sem.at[n])
        for n, (name, (src, dst)) in enumerate(parts.items())
    }
    for load in loads.values():
        load.start()

    def dev(f, r):
        return {"frame": f, "row": r}

    barrier = pltpu.get_barrier_semaphore()
    expected = jnp.int32(nf - 1)
    for step in range(1, nf):
        pl.semaphore_signal(barrier, inc=1, device_id=dev((me_f + step) % nf, me_r), device_id_type=MESH)
    row_start = my_group * group - group
    for step in range(3 * group):
        peer = row_start + step
        ok = (peer >= 0) & (peer < nr) & (peer != me_r)
        expected = expected + ok.astype(jnp.int32)

        @pl.when(ok)
        def _(peer=peer):
            pl.semaphore_signal(barrier, inc=1, device_id=dev(me_f, peer), device_id_type=MESH)

    cg[me_f] = coarse_ref[...]
    pl.semaphore_wait(barrier, expected)

    def gather_copy(step):
        return pltpu.make_async_remote_copy(
            src_ref=coarse_ref,
            dst_ref=cg.at[me_f],
            send_sem=g_send.at[step - 1],
            recv_sem=g_recv.at[step - 1],
            device_id=dev((me_f + step) % nf, me_r),
            device_id_type=MESH,
        )

    for step in range(1, nf):
        gather_copy(step).start()

    def remote(n, src, dst, f, r):
        return pltpu.make_async_remote_copy(
            src_ref=src,
            dst_ref=dst,
            send_sem=halo_send.at[n],
            recv_sem=halo_recv.at[n],
            device_id=dev(f, r),
            device_id_type=MESH,
        )

    own_f, own_r = pl.ds(1, f_dev), pl.ds(1, rows)
    cut = (rows + 1) // 2
    pieces = [(0, cut), (cut, rows - cut)]
    row_halo, frame_halo, corner_halo = [], [[], []], []
    for n, d in enumerate((-1, 1)):
        there = (me_r + d >= 0) & (me_r + d < nr)
        source = (me_r - d >= 0) & (me_r - d < nr)
        src_r, dst_r = (rows - 1, 0) if d > 0 else (0, rows_ext - 1)
        row_halo.append(
            (
                remote(n, fine_ref.at[:, pl.ds(src_r, 1)], fb.at[own_f, pl.ds(dst_r, 1)], me_f, me_r + d),
                there,
                source,
            )
        )

        @pl.when(jnp.logical_not(source))
        def _(dst_r=dst_r):
            fb[:, dst_r] = jnp.zeros((frames_ext, chans, width), BF)

        for e, at in enumerate((0, frames_ext - 1)):
            corner_halo.append(
                (
                    remote(6 + 2 * n + e, fb.at[at, src_r + 1], fb.at[at, dst_r], me_f, me_r + d),
                    there & (me_f > 0 if e == 0 else me_f < nf - 1),
                    source & (me_f > 0 if e == 0 else me_f < nf - 1),
                )
            )
        there = (me_f + d >= 0) & (me_f + d < nf)
        source = (me_f - d >= 0) & (me_f - d < nf)
        src_f, dst_f = (f_dev - 1, 0) if d > 0 else (0, frames_ext - 1)
        for piece, (start, size) in enumerate(pieces):
            if size:
                copy = remote(
                    2 + 2 * n + piece,
                    fine_ref.at[src_f, pl.ds(start, size)],
                    fb.at[dst_f, pl.ds(1 + start, size)],
                    me_f + d,
                    me_r,
                )
                frame_halo[piece].append((copy, there, source))

        @pl.when(jnp.logical_not(source))
        def _(dst_f=dst_f):
            fb[dst_f] = jnp.zeros((rows_ext, chans, width), BF)

    def start_all(copies):
        for copy, there, _ in copies:

            @pl.when(there)
            def _(copy=copy):
                copy.start()

    def arrive_all(copies):
        for copy, _, source in copies:

            @pl.when(source)
            def _(copy=copy):
                copy.wait_recv()

    def sent_all(copies):
        for copy, there, _ in copies:

            @pl.when(there)
            def _(copy=copy):
                copy.wait_send()

    start_all(frame_halo[0])
    start_all(row_halo)

    @pl.when(me_r == 0)
    def _():
        ub[1] = jnp.zeros(ub.shape[1:], BF)

    @pl.when(me_r == nr - 1)
    def _():
        ub[2] = jnp.zeros(ub.shape[1:], BF)

    gain_one[...] = jnp.broadcast_to(gain_one_ref[...][None, :], (width, chans)).T
    gain_two[...] = jnp.broadcast_to(gain_two_ref[...][None, :], (width, chans)).T

    def turn(dy):
        loads[f"space{dy}"].wait()
        cst[dy] = cs[dy].T

    turn(0)
    loads["qkv"].wait()
    for step in range(1, nf):
        gather_copy(step).wait()
    cells_all = jnp.concatenate([cg[j].astype(F32) for j in range(nf)], axis=1).astype(BF)
    qkv = []
    for i in range(3):
        product = lax.dot_general(
            cells_all, wq[i], (((1,), (1,)), ((), ())), preferred_element_type=F32
        )
        qkv.append(product.astype(BF))
    query, keys, values = qkv

    head_of_lane = lax.broadcasted_iota(jnp.int32, (cells, c_dev), 1) // HD
    spread = jnp.concatenate(
        [jnp.where(head_of_lane == h, query.astype(F32), 0.0) for h in range(heads)], axis=0
    ).astype(BF)
    scores = lax.dot_general(
        spread, keys, (((1,), (1,)), ((), ())), preferred_element_type=F32
    ) / math.sqrt(HD)
    cell_q = lax.broadcasted_iota(jnp.int32, scores.shape, 0) % p_dev
    cell_k = lax.broadcasted_iota(jnp.int32, scores.shape, 1) % p_dev
    same = cell_q == cell_k
    scores = jnp.where(same, scores, -1e30)
    top = jnp.max(scores, axis=1, keepdims=True)
    weight = jnp.where(same, jnp.exp(scores - top), 0.0)
    probs = (weight / jnp.sum(weight, axis=1, keepdims=True)).astype(BF)
    mixed = dot(probs, values)
    attn = None
    for h in range(heads):
        part = jnp.where(head_of_lane == h, mixed[h * cells : (h + 1) * cells], 0.0)
        attn = part if attn is None else attn + part
    attn = attn.astype(BF)

    loads["out"].wait()
    partial_out = dot(attn, wo[...])
    for j in range(nf):
        rs_send[j] = partial_out[:, j * c_dev : (j + 1) * c_dev].astype(BF)

    def scatter_copy(step):
        peer = (me_f + step) % nf
        return pltpu.make_async_remote_copy(
            src_ref=rs_send.at[peer],
            dst_ref=rs_recv.at[me_f],
            send_sem=r_send.at[step - 1],
            recv_sem=r_recv.at[step - 1],
            device_id=dev(peer, me_r),
            device_id_type=MESH,
        )

    for step in range(1, nf):
        scatter_copy(step).start()
    rs_recv[me_f] = rs_send[me_f]
    turn(1)
    loads["up"].wait()
    for step in range(1, nf):
        scatter_copy(step).wait()
    share = coarse_ref[...].astype(F32)
    for j in range(nf):
        share = share + rs_recv[j].astype(F32)
    up_partial = dot(share.astype(BF), wu[...]).astype(BF)

    up_send[...] = up_partial
    up_recv[me_f] = up_partial

    def sum_copy(step):
        return pltpu.make_async_remote_copy(
            src_ref=up_send,
            dst_ref=up_recv.at[me_f],
            send_sem=u_send.at[step - 1],
            recv_sem=u_recv.at[step - 1],
            device_id=dev((me_f + step) % nf, me_r),
            device_id_type=MESH,
        )

    for step in range(1, nf):
        sum_copy(step).start()
    start_all(frame_halo[1])
    turn(2)
    for step in range(1, nf):
        sum_copy(step).wait()
    up = up_recv[0].astype(F32)
    for j in range(1, nf):
        up = up + up_recv[j].astype(F32)
    up = up.astype(BF)

    ub_send[...] = up
    ub[0, k_me] = up

    def row_copy(n, region, peer):
        return pltpu.make_async_remote_copy(
            src_ref=ub_send,
            dst_ref=ub.at[region, k_me],
            send_sem=b_send.at[n],
            recv_sem=b_recv.at[region, k_me],
            device_id=dev(me_f, peer),
            device_id_type=MESH,
        )

    def row_arrival(region, k):
        return pltpu.make_async_remote_copy(
            src_ref=ub_send,
            dst_ref=ub.at[region, k],
            send_sem=b_send.at[0],
            recv_sem=b_recv.at[region, k],
            device_id=dev(me_f, me_r),
            device_id_type=MESH,
        )

    base = my_group * group
    targets = [(step - 1, 0, base + (k_me + step) % group, None) for step in range(1, group)]
    targets.append((group - 1, 1, base + group, my_group < n_groups - 1))
    targets.append((group, 2, base - 1, my_group > 0))
    for n, region, peer, ok in targets:
        if ok is None:
            row_copy(n, region, peer).start()
        else:

            @pl.when(ok)
            def _(n=n, region=region, peer=peer):
                row_copy(n, region, peer).start()

    loads["time"].wait()
    ctt[...] = ct[...].T
    span = group * cells
    lanes = frames_ext * width
    rho = lax.broadcasted_iota(jnp.int32, (span, lanes), 0)
    lane = lax.broadcasted_iota(jnp.int32, (span, lanes), 1)
    total_frames = nf * f_dev
    frame_at = me_f * f_dev - 1 + lane // width
    wanted_frame = (frame_at * cf_count + total_frames) // total_frames - 1
    wanted_cell = (lane % width) // UPSAMPLE
    frame_of = (rho % cells) // p_dev
    cell_of = (rho // cells) * p_dev + rho % p_dev
    pick = jnp.where((wanted_frame == frame_of) & (wanted_cell == cell_of), 1.0, 0.0).astype(BF)

    loads["fine"].wait()
    arrive_all(row_halo)
    for step in range(1, group):
        row_arrival(0, (k_me + step) % group).wait_recv()

    @pl.when(first & (my_group > 0))
    def _():
        for k in range(group):
            row_arrival(1, k).wait_recv()

    @pl.when(last & (my_group < n_groups - 1))
    def _():
        for k in range(group):
            row_arrival(2, k).wait_recv()

    def widened(region):
        block = [ub[region, k] for k in range(group)]
        block = jnp.concatenate(block, axis=0) if group > 1 else block[0]
        return dot_t(block, pick)

    own = widened(0)
    above = widened(jnp.where(first, 1, 0))
    below = widened(jnp.where(last, 2, 0))
    column = lax.broadcasted_iota(jnp.int32, (chans, width), 1)
    for place, t in enumerate([*range(1, frames_ext - 1), 0, frames_ext - 1]):
        if place == 1:
            arrive_all(frame_halo[0])
            arrive_all(frame_halo[1])
            start_all(corner_halo)
        if t == 0:
            arrive_all(corner_halo)
        slot = place % 2
        window = slice(t * width, (t + 1) * width)
        for r in range(rows_ext):
            spread_up = above if r == 0 else below if r == rows_ext - 1 else own
            merged = (fb[t, r].astype(F32) + spread_up[:, window]).astype(BF)
            if 0 < t < frames_ext - 1 and 0 < r < rows_ext - 1:
                fb[t, r] = merged
            v = merged.astype(F32)
            scale = lax.rsqrt(jnp.mean(v * v, axis=0, keepdims=True) + 1e-06)
            act = silu(v * scale * gain_one[...])
            here = slice(r * width, (r + 1) * width)
            x3[slot, chans : 2 * chans, here] = act.astype(BF)
            left = jnp.where(column == 0, 0.0, pltpu.roll(act, 1, 1))
            right = jnp.where(column == width - 1, 0.0, pltpu.roll(act, width - 1, 1))
            x3[slot, 0:chans, here] = left.astype(BF)
            x3[slot, 2 * chans : 3 * chans, here] = right.astype(BF)
        spatial = None
        for dy in range(3):
            term = dot(cst[dy], x3[slot, :, dy * width : (dy + rows) * width])
            spatial = term if spatial is None else spatial + term
        for r in range(rows):
            here = slice(r * width, (r + 1) * width)
            v = spatial[:, here]
            scale = lax.rsqrt(jnp.mean(v * v, axis=0, keepdims=True) + 1e-06)
            n2[t * chans : (t + 1) * chans, here] = silu(v * scale * gain_two[...]).astype(BF)
    for t in range(f_dev):
        temporal = dot(ctt[...], n2[t * chans : (t + 3) * chans, :])
        for r in range(rows):
            here = slice(r * width, (r + 1) * width)
            out_ref[t, r] = (fb[t + 1, r + 1].astype(F32) + temporal[:, here]).astype(BF)

    sent_all([*row_halo, *frame_halo[0], *frame_halo[1], *corner_halo])
    for n, region, peer, ok in targets:
        if ok is None:
            row_copy(n, region, peer).wait_send()
        else:

            @pl.when(ok)
            def _(n=n, region=region, peer=peer):
                row_copy(n, region, peer).wait_send()


def local(fine, coarse, w_qkv, w_out, w_up, gain_one, conv_space, gain_two, conv_time):
    nf = lax.axis_size("frame")
    nr = lax.axis_size("row")
    f_dev, chans, rows, width = fine.shape
    cf_count, p_dev, c_dev = coarse.shape
    cells = cf_count * p_dev
    cc = nf * c_dev
    group = (width // UPSAMPLE) // p_dev
    fine_t = jnp.transpose(fine, (0, 2, 1, 3))
    any_spec = pl.BlockSpec(memory_space=pl.ANY)
    vmem = pl.BlockSpec(memory_space=pltpu.VMEM)
    dma = pltpu.SemaphoreType.DMA
    out = pl.pallas_call(
        functools.partial(kernel, nf, nr, cf_count, p_dev),
        out_shape=jax.ShapeDtypeStruct((f_dev, rows, chans, width), BF),
        in_specs=[any_spec, vmem, any_spec, any_spec, any_spec, vmem, any_spec, vmem, any_spec],
        out_specs=vmem,
        scratch_shapes=[
            pltpu.VMEM((3, c_dev, cc), BF),
            pltpu.VMEM((c_dev, cc), BF),
            pltpu.VMEM((c_dev, chans), BF),
            pltpu.VMEM((3, 3 * chans, chans), BF),
            pltpu.VMEM((3 * chans, chans), BF),
            pltpu.VMEM((3, chans, 3 * chans), BF),
            pltpu.VMEM((chans, 3 * chans), BF),
            pltpu.VMEM((f_dev + 2, rows + 2, chans, width), BF),
            pltpu.VMEM((nf, cells, c_dev), BF),
            pltpu.VMEM((nf, cells, c_dev), BF),
            pltpu.VMEM((nf, cells, c_dev), BF),
            pltpu.VMEM((cells, chans), BF),
            pltpu.VMEM((nf, cells, chans), BF),
            pltpu.VMEM((cells, chans), BF),
            pltpu.VMEM((3, group, cells, chans), BF),
            pltpu.VMEM((2, 3 * chans, (rows + 2) * width), BF),
            pltpu.VMEM(((f_dev + 2) * chans, rows * width), BF),
            pltpu.VMEM((chans, width), F32),
            pltpu.VMEM((chans, width), F32),
            dma((8,)),
            dma((10,)),
            dma((10,)),
            dma((nf,)),
            dma((nf,)),
            dma((nf,)),
            dma((nf,)),
            dma((nf,)),
            dma((nf,)),
            dma((group + 1,)),
            dma((3, group)),
        ],
        compiler_params=pltpu.CompilerParams(
            collective_id=0, has_side_effects=True, vmem_limit_bytes=56 * 1024 * 1024
        ),
        name="decoder_window",
    )(
        fine_t,
        coarse.reshape(cells, c_dev),
        jnp.swapaxes(w_qkv, 1, 2),
        w_out,
        w_up,
        gain_one,
        conv_space.reshape(3, 3 * chans, chans),
        gain_two,
        conv_time.reshape(3 * chans, chans),
    )
    return jnp.transpose(out, (0, 2, 1, 3))


def solution(mesh):
    return jax.shard_map(
        local,
        mesh=mesh,
        in_specs=(
            P("frame", None, "row", None),
            P(None, "row", "frame"),
            P(None, None, "frame"),
            P("frame", None),
            P("frame", None),
            P(),
            P(),
            P(),
            P(),
        ),
        out_specs=P("frame", None, "row", None),
        check_vma=False,
    )
```

profile of v0, /device:TPU:11, one launch (start us, length us, event | category | flops | bytes accessed | tf_op | source)
XLA Modules:
  0.0 39.1 jit_solution(6091600755456604838)
XLA Ops:
  0.0 2.0 %copy.13 = bf16[2,320,4,128]{3,1,2,0:T(8,128)(2,1)} copy(bf16[2,320,4,128]{3,2,1,0:T(4,128)(2,1)} %param.9) | data formatting | bytes 1310720 | tf_op args[0]
  2.0 34.6 %decoder_window.1 = bf16[2,4,320,128]{3,2,1,0:T(8,128)(2,1)} custom-call(bf16[2,4,320,128]{3,2,1,0:T(8,128)(2,1)} %bitcast.9, bf16[32,320]{1,0:T(8,128)(2,1)} %bitcast.13, bf16[3,320,1280]{2,1,0:T(8,128)(2,1)} %bitcast.10, bf16[320,1280]{1,0:T(8,128)(2,1)} %w_out_ref.1, bf16[320,320]{1,0:T(8,128)(2,1)} %w_up_ref.1, f32[320]{0:T(512)} %gain_one_ref.1, ...), custom_call_target="tpu_custom_call" | custom-call | tf_op jit(solution)/shard_map/decoder_window/pallas_call | solution.py:418
  36.7 2.4 %copy.11 = bf16[2,320,4,128]{3,2,1,0:T(4,128)(2,1)} copy(bf16[2,320,4,128]{3,1,2,0:T(8,128)(2,1)} %bitcast.8) | data formatting | bytes 1310720 | tf_op jit(solution)/shard_map/transpose | solution.py:470
where the time goes:
time: 39.4 us; the launch traced here: 39.1 us
  Pallas kernels  34.6 us (88%)
  local copies, waits for them, and re-layouts  4.44 us (11%)
    pallas_call x1, Pallas kernels, local(): pl.pallas_call(functools.partial(kernel, nf, nr, cf_count, p_dev), out_sh...  34.6 us
    transpose x1, local copies, waits for them, and re-layouts, local(): return jnp.transpose(out, (0, 2, 1, 3))  2.43 us
    unnamed x1, local copies, waits for them, and re-layouts  2.01 us

commit v1 on v0

v1 whole, which is shorter than its diff:
```python
import functools
import math

import jax
import jax.numpy as jnp
from jax import lax
from jax.experimental import pallas as pl
from jax.experimental.pallas import tpu as pltpu
from jax.sharding import PartitionSpec as P

HD = 80
UPSAMPLE = 8
MESH = pl.DeviceIdType.MESH
BF = jnp.bfloat16
F32 = jnp.float32


def dot(a, b):
    return jnp.dot(a, b, preferred_element_type=F32)


def dot_t(a, b):
    return lax.dot_general(a, b, (((0,), (0,)), ((), ())), preferred_element_type=F32)


def norm_silu(v, half_gain):
    scale = lax.rsqrt(jnp.mean(v * v, axis=0, keepdims=True) + 1e-06)
    half = v * scale * half_gain
    return half + half * jnp.tanh(half)


def kernel(
    nf, nr, cf_count, p_dev, rows,
    fine_ref, coarse_ref, w_qkv_ref, w_out_ref, w_up_ref, gain_one_ref, conv_s_ref, gain_two_ref, conv_t_ref,
    out_ref,
    cv, g1, g2, ff, wq, wo, wu, cs, ct, cst, ctt, fb, mg, cg, rs_send, rs_recv, up_send, up_recv, ub, x3, n2,
    half_one, half_two, o32, ov,
    load_sem, halo_send, halo_recv, g_send, g_recv, r_send, r_recv, u_send, u_recv, b_send, b_recv, out_sem,
):
    f_dev, flat, width = fine_ref.shape
    chans = flat // rows
    cells, c_dev = coarse_ref.shape
    frames_ext = f_dev + 2
    rows_ext = rows + 2
    group = (width // UPSAMPLE) // p_dev
    n_groups = nr // group
    heads = c_dev // HD
    span = group * p_dev
    total_frames = nf * f_dev
    me_f = lax.axis_index("frame")
    me_r = lax.axis_index("row")
    my_group = me_r // group
    k_me = me_r % group
    base = my_group * group
    first = k_me == 0
    last = k_me == group - 1
    has_above = first & (my_group > 0)
    has_below = last & (my_group < n_groups - 1)

    def dev(f, r):
        return {"frame": f, "row": r}

    barrier = pltpu.get_barrier_semaphore()
    for step_f in range(nf):
        for step_k in range(group):
            if step_f or step_k:
                peer = dev((me_f + step_f) % nf, base + (k_me + step_k) % group)
                pl.semaphore_signal(barrier, inc=1, device_id=peer, device_id_type=MESH)
    expected = jnp.int32(nf * group - 1)
    for ok, peer in ((has_above, me_r - 1), (has_below, me_r + 1)):
        expected = expected + ok.astype(jnp.int32)

        @pl.when(ok)
        def _(peer=peer):
            pl.semaphore_signal(barrier, inc=1, device_id=dev(me_f, peer), device_id_type=MESH)

    parts = {
        "coarse": (coarse_ref, cv),
        "fine": (fine_ref, ff),
        "gain_one": (gain_one_ref, g1),
        "gain_two": (gain_two_ref, g2),
        "qkv": (w_qkv_ref, wq),
        "out": (w_out_ref, wo),
        "space0": (conv_s_ref.at[0], cs.at[0]),
        "up": (w_up_ref, wu),
        "space1": (conv_s_ref.at[1], cs.at[1]),
        "space2": (conv_s_ref.at[2], cs.at[2]),
        "time": (conv_t_ref, ct),
    }
    loads = {
        name: pltpu.make_async_copy(src, dst, load_sem.at[n])
        for n, (name, (src, dst)) in enumerate(parts.items())
    }
    for load in loads.values():
        load.start()

    def gather_copy(step):
        return pltpu.make_async_remote_copy(
            src_ref=cv,
            dst_ref=cg.at[me_f],
            send_sem=g_send.at[step - 1],
            recv_sem=g_recv.at[step - 1],
            device_id=dev((me_f + step) % nf, me_r),
            device_id_type=MESH,
        )

    loads["coarse"].wait()
    pl.semaphore_wait(barrier, expected)
    for step in range(1, nf):
        gather_copy(step).start()
    cg[me_f] = cv[...]

    loads["fine"].wait()
    block = math.gcd(chans, 64)
    size = block * rows
    i = lax.broadcasted_iota(jnp.int32, (size, size), 0)
    k = lax.broadcasted_iota(jnp.int32, (size, size), 1)
    sort_rows = jnp.where((k % rows == i // block) & (k // rows == i % block), 1.0, 0.0).astype(BF)
    for b in range(chans // block):
        mixed_rows = jnp.concatenate([ff[t, b * size : (b + 1) * size, :] for t in range(f_dev)], axis=1)
        sorted_rows = dot(sort_rows, mixed_rows).astype(BF)
        for t in range(f_dev):
            for r in range(rows):
                fb[1 + t, 1 + r, b * block : (b + 1) * block, :] = sorted_rows[
                    r * block : (r + 1) * block, t * width : (t + 1) * width
                ]

    def remote(n, src, dst, f, r):
        return pltpu.make_async_remote_copy(
            src_ref=src,
            dst_ref=dst,
            send_sem=halo_send.at[n],
            recv_sem=halo_recv.at[n],
            device_id=dev(f, r),
            device_id_type=MESH,
        )

    own_f = pl.ds(1, f_dev)
    row_order = [0, rows - 1, *range(1, rows - 1)] if rows > 1 else [0]
    row_halo, corner_halo = [], []
    frame_halo = [[] for _ in row_order]
    at_frame = ((0, me_f > 0), (frames_ext - 1, me_f < nf - 1))
    n_sem = 0
    for d in (-1, 1):
        there = (me_r + d >= 0) & (me_r + d < nr)
        source = (me_r - d >= 0) & (me_r - d < nr)
        src_r, dst_r = (rows, 0) if d > 0 else (1, rows_ext - 1)
        row_halo.append(
            (remote(n_sem, fb.at[own_f, src_r], fb.at[own_f, dst_r], me_f, me_r + d), there, source)
        )
        n_sem += 1
        for at, exists in at_frame:
            corner_halo.append(
                (remote(n_sem, fb.at[at, src_r], fb.at[at, dst_r], me_f, me_r + d), there & exists, source & exists)
            )
            n_sem += 1
    for d in (-1, 1):
        there = (me_f + d >= 0) & (me_f + d < nf)
        source = (me_f - d >= 0) & (me_f - d < nf)
        src_f, dst_f = (f_dev, 0) if d > 0 else (1, frames_ext - 1)
        for place, r in enumerate(row_order):
            copy = remote(n_sem, fb.at[src_f, 1 + r], fb.at[dst_f, 1 + r], me_f + d, me_r)
            frame_halo[place].append((copy, there, source))
            n_sem += 1

    def start_all(copies):
        for copy, there, _ in copies:

            @pl.when(there)
            def _(copy=copy):
                copy.start()

    def arrive_all(copies):
        for copy, _, source in copies:

            @pl.when(source)
            def _(copy=copy):
                copy.wait_recv()

    def sent_all(copies):
        for copy, there, _ in copies:

            @pl.when(there)
            def _(copy=copy):
                copy.wait_send()

    start_all(row_halo)
    start_all(frame_halo[0])
    if rows > 1:
        start_all(frame_halo[1])

    for edge, at in ((me_r == 0, 0), (me_r == nr - 1, rows_ext - 1)):

        @pl.when(edge)
        def _(at=at):
            fb[:, at] = jnp.zeros((frames_ext, chans, width), BF)

    for edge, at in ((me_f == 0, 0), (me_f == nf - 1, frames_ext - 1)):

        @pl.when(edge)
        def _(at=at):
            fb[at] = jnp.zeros((rows_ext, chans, width), BF)

    for edge, region in ((first & (my_group == 0), 1), (last & (my_group == n_groups - 1), 2)):

        @pl.when(edge)
        def _(region=region):
            ub[:, region] = jnp.zeros((3, span, chans), BF)

    for edge, slot in ((me_f == 0, 1), (me_f == nf - 1, 2)):

        @pl.when(edge)
        def _(slot=slot):
            ub[slot] = jnp.zeros((3, span, chans), BF)

    loads["gain_one"].wait()
    loads["gain_two"].wait()
    half_one[...] = jnp.broadcast_to(0.5 * g1[...][None, :], (width, chans)).T
    half_two[...] = jnp.broadcast_to(0.5 * g2[...][None, :], (width, chans)).T

    def turn(dy):
        loads[f"space{dy}"].wait()
        cst[dy] = cs[dy].T

    loads["qkv"].wait()
    turn(0)
    for step in range(1, nf):
        gather_copy(step).wait()
    cells_all = jnp.concatenate([cg[j].astype(F32) for j in range(nf)], axis=1).astype(BF)
    qkv = []
    for i in range(3):
        product = lax.dot_general(
            cells_all, wq[i], (((1,), (1,)), ((), ())), preferred_element_type=F32
        )
        qkv.append(product.astype(BF))
    query, keys, values = qkv

    head_of_lane = lax.broadcasted_iota(jnp.int32, (cells, c_dev), 1) // HD
    spread = jnp.concatenate(
        [jnp.where(head_of_lane == h, query.astype(F32), 0.0) for h in range(heads)], axis=0
    ).astype(BF)
    scores = lax.dot_general(
        spread, keys, (((1,), (1,)), ((), ())), preferred_element_type=F32
    ) / math.sqrt(HD)
    cell_q = lax.broadcasted_iota(jnp.int32, scores.shape, 0) % p_dev
    cell_k = lax.broadcasted_iota(jnp.int32, scores.shape, 1) % p_dev
    same = cell_q == cell_k
    scores = jnp.where(same, scores, -1e30)
    top = jnp.max(scores, axis=1, keepdims=True)
    weight = jnp.where(same, jnp.exp(scores - top), 0.0)
    probs = (weight / jnp.sum(weight, axis=1, keepdims=True)).astype(BF)
    mixed = dot(probs, values)
    attn = None
    for h in range(heads):
        part = jnp.where(head_of_lane == h, mixed[h * cells : (h + 1) * cells], 0.0)
        attn = part if attn is None else attn + part
    attn = attn.astype(BF)

    loads["out"].wait()
    partial_out = dot(attn, wo[...])
    for j in range(nf):
        rs_send[j] = partial_out[:, j * c_dev : (j + 1) * c_dev].astype(BF)

    def scatter_copy(step):
        peer = (me_f + step) % nf
        return pltpu.make_async_remote_copy(
            src_ref=rs_send.at[peer],
            dst_ref=rs_recv.at[me_f],
            send_sem=r_send.at[step - 1],
            recv_sem=r_recv.at[step - 1],
            device_id=dev(peer, me_r),
            device_id_type=MESH,
        )

    for step in range(1, nf):
        scatter_copy(step).start()
    if rows > 2:
        start_all(frame_halo[2])
    rs_recv[me_f] = rs_send[me_f]
    turn(1)
    loads["up"].wait()
    for step in range(1, nf):
        scatter_copy(step).wait()
    share = cv[...].astype(F32)
    for j in range(nf):
        share = share + rs_recv[j].astype(F32)
    up_partial = dot(share.astype(BF), wu[...])
    for j in range(cf_count):
        up_send[j] = up_partial[j * p_dev : (j + 1) * p_dev].astype(BF)

    def coarse_frame(f):
        return (f * f_dev * cf_count) // total_frames

    def sum_copy(step_f, step_k):
        peer = (me_f + step_f) % nf
        return pltpu.make_async_remote_copy(
            src_ref=up_send.at[coarse_frame(peer)],
            dst_ref=up_recv.at[k_me, me_f],
            send_sem=u_send.at[step_f, step_k],
            recv_sem=u_recv.at[step_f, step_k],
            device_id=dev(peer, base + (k_me + step_k) % group),
            device_id_type=MESH,
        )

    sums = [(a, b) for a in range(nf) for b in range(group) if a or b]
    for a, b in sums[::-1]:
        sum_copy(a, b).start()
    up_recv[k_me, me_f] = up_send[coarse_frame(me_f)]
    for place in range(3, rows):
        start_all(frame_halo[place])
    arrive_all(frame_halo[0])
    if rows > 1:
        arrive_all(frame_halo[1])
    start_all(corner_halo)
    turn(2)
    loads["time"].wait()
    ctt[...] = ct[...].T
    rho = lax.broadcasted_iota(jnp.int32, (span, width), 0)
    lane = lax.broadcasted_iota(jnp.int32, (span, width), 1)
    pick = jnp.where(lane // UPSAMPLE == rho, 1.0, 0.0).astype(BF)
    for a, b in sums:
        sum_copy(a, b).wait()
    halves = []
    for c in range(group):
        up = up_recv[c, 0].astype(F32)
        for j in range(1, nf):
            up = up + up_recv[c, j].astype(F32)
        halves.append(up)
    ub[0, 0] = (jnp.concatenate(halves, axis=0) if group > 1 else halves[0]).astype(BF)

    def block_copy(n, src, slot, region, f, r):
        return pltpu.make_async_remote_copy(
            src_ref=ub.at[0, src],
            dst_ref=ub.at[slot, region],
            send_sem=b_send.at[n],
            recv_sem=b_recv.at[slot, region],
            device_id=dev(f, r),
            device_id_type=MESH,
        )

    edges = [
        (block_copy(0, 0, 0, 1, me_f, me_r + 1), has_below, has_above),
        (block_copy(1, 0, 0, 2, me_f, me_r - 1), has_above, has_below),
    ]
    beside = []
    n_block = 2
    for slot, d in ((1, 1), (2, -1)):
        there = (me_f + d >= 0) & (me_f + d < nf)
        source = (me_f - d >= 0) & (me_f - d < nf)
        for region, have in ((0, None), (1, has_above), (2, has_below)):
            copy = block_copy(n_block, region, slot, region, me_f + d, me_r)
            n_block += 1
            beside.append((copy, there, source) if have is None else (copy, there & have, source & have))
    start_all(edges)
    start_all(beside[::3])

    lane_bf = lax.broadcasted_iota(jnp.int32, (chans, width), 1)
    keep_left = jnp.where(lane_bf == 0, 0.0, 1.0).astype(BF)
    keep_right = jnp.where(lane_bf == width - 1, 0.0, 1.0).astype(BF)

    def activate(t, r, widened):
        v = fb[t, r].astype(F32) + widened
        if 0 < t < frames_ext - 1 and 0 < r < rows_ext - 1:
            mg[t - 1, r - 1] = v.astype(BF)
        act = norm_silu(v, half_one[...]).astype(BF)
        here = slice(r * width, (r + 1) * width)
        x3[t, chans : 2 * chans, here] = act
        x3[t, 0:chans, here] = pltpu.roll(act, 1, 1) * keep_left
        x3[t, 2 * chans : 3 * chans, here] = pltpu.roll(act, width - 1, 1) * keep_right

    def convolve(t):
        spatial = None
        for dy in range(3):
            term = dot(cst[dy], x3[t, :, dy * width : (dy + rows) * width])
            spatial = term if spatial is None else spatial + term
        for r in range(rows):
            here = slice(r * width, (r + 1) * width)
            n2[t * chans : (t + 1) * chans, here] = norm_silu(spatial[:, here], half_two[...]).astype(BF)

    own = dot_t(ub[0, 0], pick)
    for t in range(1, frames_ext - 1):
        for r in range(1, rows_ext - 1):
            activate(t, r, own)
    arrive_all(edges)
    start_all(beside[1::3])
    start_all(beside[2::3])
    arrive_all(row_halo)
    above = dot_t(ub[0, jnp.where(first, 1, 0)], pick)
    below = dot_t(ub[0, jnp.where(last, 2, 0)], pick)
    for t in range(1, frames_ext - 1):
        activate(t, 0, above)
        activate(t, rows_ext - 1, below)
    for t in range(1, frames_ext - 1):
        convolve(t)
    for place in range(2, rows):
        arrive_all(frame_halo[place])
    arrive_all(beside)
    arrive_all(corner_halo)
    for t, slot in ((0, 1), (frames_ext - 1, 2)):
        own = dot_t(ub[slot, 0], pick)
        above = dot_t(ub[slot, jnp.where(first, 1, 0)], pick)
        below = dot_t(ub[slot, jnp.where(last, 2, 0)], pick)
        for r in range(rows_ext):
            activate(t, r, above if r == 0 else below if r == rows_ext - 1 else own)
        convolve(t)
    outs = []
    for t in range(f_dev):
        temporal = dot(ctt[...], n2[t * chans : (t + 3) * chans, :])
        for r in range(rows):
            here = slice(r * width, (r + 1) * width)
            o32[t, pl.ds(r, chans, rows), :] = mg[t, r].astype(F32) + temporal[:, here]
        ov[t] = o32[t].astype(BF)
        outs.append(pltpu.make_async_copy(ov.at[t], out_ref.at[t], out_sem.at[t]))
        outs[t].start()

    for copies in (row_halo, *frame_halo, corner_halo, edges, beside):
        sent_all(copies)
    for copy in outs:
        copy.wait()


def local(fine, coarse, w_qkv, w_out, w_up, gain_one, conv_space, gain_two, conv_time):
    nf = lax.axis_size("frame")
    nr = lax.axis_size("row")
    f_dev, chans, rows, width = fine.shape
    cf_count, p_dev, c_dev = coarse.shape
    cells = cf_count * p_dev
    cc = nf * c_dev
    group = (width // UPSAMPLE) // p_dev
    span = group * p_dev
    any_spec = pl.BlockSpec(memory_space=pl.ANY)
    dma = pltpu.SemaphoreType.DMA
    n_halo = 2 * (1 + 2) + 2 * rows
    out = pl.pallas_call(
        functools.partial(kernel, nf, nr, cf_count, p_dev, rows),
        out_shape=jax.ShapeDtypeStruct((f_dev, chans * rows, width), BF),
        in_specs=[any_spec] * 9,
        out_specs=any_spec,
        scratch_shapes=[
            pltpu.VMEM((cells, c_dev), BF),
            pltpu.VMEM((chans,), F32),
            pltpu.VMEM((chans,), F32),
            pltpu.VMEM((f_dev, chans * rows, width), BF),
            pltpu.VMEM((3, c_dev, cc), BF),
            pltpu.VMEM((c_dev, cc), BF),
            pltpu.VMEM((c_dev, chans), BF),
            pltpu.VMEM((3, 3 * chans, chans), BF),
            pltpu.VMEM((3 * chans, chans), BF),
            pltpu.VMEM((3, chans, 3 * chans), BF),
            pltpu.VMEM((chans, 3 * chans), BF),
            pltpu.VMEM((f_dev + 2, rows + 2, chans, width), BF),
            pltpu.VMEM((f_dev, rows, chans, width), BF),
            pltpu.VMEM((nf, cells, c_dev), BF),
            pltpu.VMEM((nf, cells, c_dev), BF),
            pltpu.VMEM((nf, cells, c_dev), BF),
            pltpu.VMEM((cf_count, p_dev, chans), BF),
            pltpu.VMEM((group, nf, p_dev, chans), BF),
            pltpu.VMEM((3, 3, span, chans), BF),
            pltpu.VMEM((f_dev + 2, 3 * chans, (rows + 2) * width), BF),
            pltpu.VMEM(((f_dev + 2) * chans, rows * width), BF),
            pltpu.VMEM((chans, width), F32),
            pltpu.VMEM((chans, width), F32),
            pltpu.VMEM((f_dev, chans * rows, width), F32),
            pltpu.VMEM((f_dev, chans * rows, width), BF),
            dma((11,)),
            dma((n_halo,)),
            dma((n_halo,)),
            dma((nf,)),
            dma((nf,)),
            dma((nf,)),
            dma((nf,)),
            dma((nf, group)),
            dma((nf, group)),
            dma((8,)),
            dma((3, 3)),
            dma((f_dev,)),
        ],
        compiler_params=pltpu.CompilerParams(
            collective_id=0, has_side_effects=True, vmem_limit_bytes=56 * 1024 * 1024
        ),
        name="decoder_window",
    )(
        fine.reshape(f_dev, chans * rows, width),
        coarse.reshape(cells, c_dev),
        jnp.swapaxes(w_qkv, 1, 2),
        w_out,
        w_up,
        gain_one,
        conv_space.reshape(3, 3 * chans, chans),
        gain_two,
        conv_time.reshape(3 * chans, chans),
    )
    return out.reshape(f_dev, chans, rows, width)


def solution(mesh):
    return jax.shard_map(
        local,
        mesh=mesh,
        in_specs=(
            P("frame", None, "row", None),
            P(None, "row", "frame"),
            P(None, None, "frame"),
            P("frame", None),
            P("frame", None),
            P(),
            P(),
            P(),
            P(),
        ),
        out_specs=P("frame", None, "row", None),
        check_vma=False,
    )
```

time: 39.4 us -> 32.8 us (0.83)
  the two profiles are of different devices: /device:TPU:11 before, /device:TPU:1 now
where the time goes in v1:
time: 32.8 us; the launch traced here: 32.6 us
  Pallas kernels  30.4 us (93%)
  local copies, waits for them, and re-layouts  2.15 us (7%)
    pallas_call x1, Pallas kernels, local(): pl.pallas_call(functools.partial(kernel, nf, nr, cf_count, p_dev, rows),...  30.4 us
    unnamed x1, local copies, waits for them, and re-layouts  2.15 us

profile of v1, /device:TPU:1, one launch (start us, length us, event | category | flops | bytes accessed | tf_op | source)
XLA Modules:
  0.0 32.6 jit_solution(6180818384716673119)
XLA Ops:
  0.0 30.4 %decoder_window.1 = bf16[2,1280,128]{2,1,0:T(8,128)(2,1)} custom-call(bf16[2,1280,128]{2,1,0:T(8,128)(2,1)} %bitcast.10, bf16[32,320]{1,0:T(8,128)(2,1)} %bitcast.11, bf16[3,320,1280]{2,1,0:T(8,128)(2,1)} %bitcast.7, bf16[320,1280]{1,0:T(8,128)(2,1)} %w_out_ref.1, bf16[320,320]{1,0:T(8,128)(2,1)} %w_up_ref.1, f32[320]{0:T(512)} %gain_one_ref.1, ...), custom_call_target="tpu_custom_call" | custom-call | tf_op jit(solution)/shard_map/decoder_window/pallas_call | solution.py:434
  30.5 2.1 %copy.11 = bf16[2,320,4,128]{3,2,1,0:T(4,128)(2,1)} copy(bf16[2,320,4,128]{3,2,1,0:T(4,128)(2,1)} %bitcast.6) | data formatting | bytes 1310720

commit v2 on v1

--- a/solution.py
+++ b/solution.py
@@ -34,8 +34,8 @@
     fine_ref, coarse_ref, w_qkv_ref, w_out_ref, w_up_ref, gain_one_ref, conv_s_ref, gain_two_ref, conv_t_ref,
     out_ref,
     cv, g1, g2, ff, wq, wo, wu, cs, ct, cst, ctt, fb, mg, cg, rs_send, rs_recv, up_send, up_recv, ub, x3, n2,
-    half_one, half_two, o32, ov,
-    load_sem, halo_send, halo_recv, g_send, g_recv, r_send, r_recv, u_send, u_recv, b_send, b_recv, out_sem,
+    half_one, half_two, o32,
+    load_sem, halo_send, halo_recv, g_send, g_recv, r_send, r_recv, u_send, u_recv, b_send, b_recv,
 ):
     f_dev, flat, width = fine_ref.shape
     chans = flat // rows
@@ -403,20 +403,15 @@
         for r in range(rows_ext):
             activate(t, r, above if r == 0 else below if r == rows_ext - 1 else own)
         convolve(t)
-    outs = []
     for t in range(f_dev):
         temporal = dot(ctt[...], n2[t * chans : (t + 3) * chans, :])
         for r in range(rows):
             here = slice(r * width, (r + 1) * width)
             o32[t, pl.ds(r, chans, rows), :] = mg[t, r].astype(F32) + temporal[:, here]
-        ov[t] = o32[t].astype(BF)
-        outs.append(pltpu.make_async_copy(ov.at[t], out_ref.at[t], out_sem.at[t]))
-        outs[t].start()
+        out_ref[t] = o32[t].astype(BF)
 
     for copies in (row_halo, *frame_halo, corner_halo, edges, beside):
         sent_all(copies)
-    for copy in outs:
-        copy.wait()
 
 
 def local(fine, coarse, w_qkv, w_out, w_up, gain_one, conv_space, gain_two, conv_time):
@@ -433,9 +428,9 @@
     n_halo = 2 * (1 + 2) + 2 * rows
     out = pl.pallas_call(
         functools.partial(kernel, nf, nr, cf_count, p_dev, rows),
-        out_shape=jax.ShapeDtypeStruct((f_dev, chans * rows, width), BF),
+        out_shape=pltpu.VMEM((f_dev, chans * rows, width), BF),
         in_specs=[any_spec] * 9,
-        out_specs=any_spec,
+        out_specs=pl.BlockSpec(memory_space=pltpu.VMEM),
         scratch_shapes=[
             pltpu.VMEM((cells, c_dev), BF),
             pltpu.VMEM((chans,), F32),
@@ -461,7 +456,6 @@
             pltpu.VMEM((chans, width), F32),
             pltpu.VMEM((chans, width), F32),
             pltpu.VMEM((f_dev, chans * rows, width), F32),
-            pltpu.VMEM((f_dev, chans * rows, width), BF),
             dma((11,)),
             dma((n_halo,)),
             dma((n_halo,)),
@@ -473,7 +467,6 @@
             dma((nf, group)),
             dma((8,)),
             dma((3, 3)),
-            dma((f_dev,)),
         ],
         compiler_params=pltpu.CompilerParams(
             collective_id=0, has_side_effects=True, vmem_limit_bytes=56 * 1024 * 1024

time: 32.8 us -> 30.7 us (0.936)
  local copies, waits for them, and re-layouts: 2.15 us -> 0.84 us
  Pallas kernels: 30.4 us -> 29.7 us
    unnamed x1, local copies, waits for them, and re-layouts: 2.15 us -> 0.84 us
    pallas_call x1, Pallas kernels: 30.4 us -> 29.7 us  [local(): pl.pallas_call(functools.partial(kernel, nf, nr, cf_count, p_dev, rows),...]
where the time goes in v2:
time: 30.7 us; the launch traced here: 30.6 us
  Pallas kernels  29.7 us (97%)
  local copies, waits for them, and re-layouts  0.84 us (3%)
    pallas_call x1, Pallas kernels, local(): pl.pallas_call(functools.partial(kernel, nf, nr, cf_count, p_dev, rows),...  29.7 us
    unnamed x1, local copies, waits for them, and re-layouts  0.84 us

profile of v2, /device:TPU:1, one launch (start us, length us, event | category | flops | bytes accessed | tf_op | source)
XLA Modules:
  0.0 30.6 jit_solution(9823521555474768676)
XLA Ops:
  0.0 29.7 %decoder_window.1 = bf16[2,1280,128]{2,1,0:T(8,128)(2,1)S(1)} custom-call(bf16[2,1280,128]{2,1,0:T(8,128)(2,1)} %bitcast.10, bf16[32,320]{1,0:T(8,128)(2,1)} %bitcast.11, bf16[3,320,1280]{2,1,0:T(8,128)(2,1)} %bitcast.7, bf16[320,1280]{1,0:T(8,128)(2,1)} %w_out_ref.1, bf16[320,320]{1,0:T(8,128)(2,1)} %w_up_ref.1, f32[320]{0:T(512)} %gain_one_ref.1, ...), custom_call_target="tpu_custom_call" | custom-call | tf_op jit(solution)/shard_map/decoder_window/pallas_call | solution.py:429
  29.7 0.8 %copy.11 = bf16[2,320,4,128]{3,2,1,0:T(4,128)(2,1)} copy(bf16[2,320,4,128]{3,2,1,0:T(4,128)(2,1)S(1)} %bitcast.6) | data formatting | bytes 1310720

commit v3 on v2

--- a/solution.py
+++ b/solution.py
@@ -33,7 +33,7 @@
     nf, nr, cf_count, p_dev, rows,
     fine_ref, coarse_ref, w_qkv_ref, w_out_ref, w_up_ref, gain_one_ref, conv_s_ref, gain_two_ref, conv_t_ref,
     out_ref,
-    cv, g1, g2, ff, wq, wo, wu, cs, ct, cst, ctt, fb, mg, cg, rs_send, rs_recv, up_send, up_recv, ub, x3, n2,
+    cv, g1, g2, ff, wq, wo, wu, cs, ct, wt, fb, mg, cg, rs_send, rs_recv, up_send, up_recv, ub, x3, n2, keep, acc,
     half_one, half_two, o32,
     load_sem, halo_send, halo_recv, g_send, g_recv, r_send, r_recv, u_send, u_recv, b_send, b_recv,
 ):
@@ -94,20 +94,48 @@
     for load in loads.values():
         load.start()
 
-    def gather_copy(step):
-        return pltpu.make_async_remote_copy(
+    def start_all(copies):
+        for copy, there, _ in copies:
+
+            @pl.when(there)
+            def _(copy=copy):
+                copy.start()
+
+    def arrive_all(copies):
+        for copy, _, source in copies:
+
+            @pl.when(source)
+            def _(copy=copy):
+                copy.wait_recv()
+
+    def sent_all(copies):
+        for copy, there, _ in copies:
+
+            @pl.when(there)
+            def _(copy=copy):
+                copy.wait_send()
+
+    def over_frames(make):
+        copies = []
+        for n, (far, d) in enumerate((far, d) for far in range(nf - 1, 0, -1) for d in (-1, 1)):
+            there = (me_f + d * far >= 0) & (me_f + d * far < nf)
+            source = (me_f - d * far >= 0) & (me_f - d * far < nf)
+            copies.append((make(n, (me_f + d * far + nf) % nf), there, source))
+        return copies
+
+    gather = over_frames(
+        lambda n, peer: pltpu.make_async_remote_copy(
             src_ref=cv,
             dst_ref=cg.at[me_f],
-            send_sem=g_send.at[step - 1],
-            recv_sem=g_recv.at[step - 1],
-            device_id=dev((me_f + step) % nf, me_r),
+            send_sem=g_send.at[n],
+            recv_sem=g_recv.at[n],
+            device_id=dev(peer, me_r),
             device_id_type=MESH,
         )
-
+    )
     loads["coarse"].wait()
     pl.semaphore_wait(barrier, expected)
-    for step in range(1, nf):
-        gather_copy(step).start()
+    start_all(gather)
     cg[me_f] = cv[...]
 
     loads["fine"].wait()
@@ -163,28 +191,6 @@
             frame_halo[place].append((copy, there, source))
             n_sem += 1
 
-    def start_all(copies):
-        for copy, there, _ in copies:
-
-            @pl.when(there)
-            def _(copy=copy):
-                copy.start()
-
-    def arrive_all(copies):
-        for copy, _, source in copies:
-
-            @pl.when(source)
-            def _(copy=copy):
-                copy.wait_recv()
-
-    def sent_all(copies):
-        for copy, there, _ in copies:
-
-            @pl.when(there)
-            def _(copy=copy):
-                copy.wait_send()
-
-    start_all(row_halo)
     start_all(frame_halo[0])
     if rows > 1:
         start_all(frame_halo[1])
@@ -218,14 +224,19 @@
     half_one[...] = jnp.broadcast_to(0.5 * g1[...][None, :], (width, chans)).T
     half_two[...] = jnp.broadcast_to(0.5 * g2[...][None, :], (width, chans)).T
 
-    def turn(dy):
-        loads[f"space{dy}"].wait()
-        cst[dy] = cs[dy].T
+    pieces = [(start, min(width, 3 * chans - start)) for start in range(0, 3 * chans, width)]
+
+    def lay(n, weights):
+        for piece, (start, size) in enumerate(pieces):
+            wt[n, piece, :, 0:size] = weights[start : start + size].T
+
+    def wide(ref, n):
+        return jnp.concatenate([ref[n, piece, :, 0:size] for piece, (_, size) in enumerate(pieces)], axis=1)
 
     loads["qkv"].wait()
-    turn(0)
-    for step in range(1, nf):
-        gather_copy(step).wait()
+    loads["space0"].wait()
+    lay(0, cs[0])
+    arrive_all(gather)
     cells_all = jnp.concatenate([cg[j].astype(F32) for j in range(nf)], axis=1).astype(BF)
     qkv = []
     for i in range(3):
@@ -261,26 +272,25 @@
     for j in range(nf):
         rs_send[j] = partial_out[:, j * c_dev : (j + 1) * c_dev].astype(BF)
 
-    def scatter_copy(step):
-        peer = (me_f + step) % nf
-        return pltpu.make_async_remote_copy(
+    scatter = over_frames(
+        lambda n, peer: pltpu.make_async_remote_copy(
             src_ref=rs_send.at[peer],
             dst_ref=rs_recv.at[me_f],
-            send_sem=r_send.at[step - 1],
-            recv_sem=r_recv.at[step - 1],
+            send_sem=r_send.at[n],
+            recv_sem=r_recv.at[n],
             device_id=dev(peer, me_r),
             device_id_type=MESH,
         )
-
-    for step in range(1, nf):
-        scatter_copy(step).start()
-    if rows > 2:
-        start_all(frame_halo[2])
+    )
+    start_all(scatter)
+    start_all(row_halo)
     rs_recv[me_f] = rs_send[me_f]
-    turn(1)
+    loads["space1"].wait()
+    loads["space2"].wait()
+    lay(1, ((cs[0].astype(F32) + cs[2].astype(F32) + cs[1].astype(F32)) * 0.5).astype(BF))
+    lay(3, cs[2])
     loads["up"].wait()
-    for step in range(1, nf):
-        scatter_copy(step).wait()
+    arrive_all(scatter)
     share = cv[...].astype(F32)
     for j in range(nf):
         share = share + rs_recv[j].astype(F32)
@@ -291,35 +301,39 @@
     def coarse_frame(f):
         return (f * f_dev * cf_count) // total_frames
 
-    def sum_copy(step_f, step_k):
-        peer = (me_f + step_f) % nf
+    def sum_copy(n, step_k, peer):
         return pltpu.make_async_remote_copy(
             src_ref=up_send.at[coarse_frame(peer)],
             dst_ref=up_recv.at[k_me, me_f],
-            send_sem=u_send.at[step_f, step_k],
-            recv_sem=u_recv.at[step_f, step_k],
+            send_sem=u_send.at[n, step_k],
+            recv_sem=u_recv.at[n, step_k],
             device_id=dev(peer, base + (k_me + step_k) % group),
             device_id_type=MESH,
         )
 
-    sums = [(a, b) for a in range(nf) for b in range(group) if a or b]
-    for a, b in sums[::-1]:
-        sum_copy(a, b).start()
+    sums = [copy for step_k in range(group) for copy in over_frames(lambda n, peer: sum_copy(n, step_k, peer))]
+    sums = [sums[n + step_k * len(scatter)] for n in range(len(scatter)) for step_k in range(group)]
+    for copy in sums:
+        start_all([copy])
+    across = [sum_copy(len(scatter), step_k, me_f) for step_k in range(1, group)]
+    for copy in across:
+        copy.start()
     up_recv[k_me, me_f] = up_send[coarse_frame(me_f)]
-    for place in range(3, rows):
+    for place in range(2, rows):
         start_all(frame_halo[place])
     arrive_all(frame_halo[0])
     if rows > 1:
         arrive_all(frame_halo[1])
     start_all(corner_halo)
-    turn(2)
+    lay(2, ((cs[0].astype(F32) + cs[2].astype(F32) - cs[1].astype(F32)) * 0.5).astype(BF))
     loads["time"].wait()
-    ctt[...] = ct[...].T
+    lay(4, ct[...])
     rho = lax.broadcasted_iota(jnp.int32, (span, width), 0)
     lane = lax.broadcasted_iota(jnp.int32, (span, width), 1)
     pick = jnp.where(lane // UPSAMPLE == rho, 1.0, 0.0).astype(BF)
-    for a, b in sums:
-        sum_copy(a, b).wait()
+    arrive_all(sums)
+    for copy in across:
+        copy.wait_recv()
     halves = []
     for c in range(group):
         up = up_recv[c, 0].astype(F32)
@@ -358,60 +372,129 @@
     keep_left = jnp.where(lane_bf == 0, 0.0, 1.0).astype(BF)
     keep_right = jnp.where(lane_bf == width - 1, 0.0, 1.0).astype(BF)
 
+    tiles = rows // 2
+
     def activate(t, r, widened):
         v = fb[t, r].astype(F32) + widened
         if 0 < t < frames_ext - 1 and 0 < r < rows_ext - 1:
             mg[t - 1, r - 1] = v.astype(BF)
-        act = norm_silu(v, half_one[...]).astype(BF)
-        here = slice(r * width, (r + 1) * width)
-        x3[t, chans : 2 * chans, here] = act
-        x3[t, 0:chans, here] = pltpu.roll(act, 1, 1) * keep_left
-        x3[t, 2 * chans : 3 * chans, here] = pltpu.roll(act, width - 1, 1) * keep_right
-
-    def convolve(t):
-        spatial = None
-        for dy in range(3):
-            term = dot(cst[dy], x3[t, :, dy * width : (dy + rows) * width])
-            spatial = term if spatial is None else spatial + term
+        return norm_silu(v, half_one[...])
+
+    def put(t, n, tile, v):
+        v = v.astype(BF)
+        x3[t, n, tile, chans : 2 * chans] = v
+        x3[t, n, tile, 0:chans] = pltpu.roll(v, 1, 1) * keep_left
+        x3[t, n, tile, 2 * chans : 3 * chans] = pltpu.roll(v, width - 1, 1) * keep_right
+
+    def product(t, n):
+        return dot(wide(wt, n), jnp.concatenate([x3[t, n, tile] for tile in range(tiles)], axis=1))
+
+    act, term = {}, {}
+
+    def rows_in(t, widened):
+        def one(tile):
+            r = 2 * tile + 1
+            act[t, r] = activate(t, r, widened)
+            act[t, r + 1] = activate(t, r + 1, widened)
+            put(t, 1, tile, act[t, r] + act[t, r + 1])
+            put(t, 2, tile, act[t, r + 1] - act[t, r])
+            if tile > 0:
+                put(t, 0, tile, act[t, r - 1] - act[t, r + 1])
+                put(t, 3, tile - 1, act[t, r - 2] - act[t, r])
+            if r + 1 == 2:
+                keep[t, 0] = act[t, 2]
+            if tile == tiles - 1:
+                keep[t, 1] = act[t, rows - 1]
+
+        return [functools.partial(one, tile) for tile in range(tiles)]
+
+    def multiply(t, n):
+        term[t, n] = product(t, n)
+        if n == 2:
+            acc[t, 0] = term[t, 1] + term[t, 2]
+            acc[t, 1] = term[t, 1] - term[t, 2]
+
+    def products(t, *which):
+        return [functools.partial(multiply, t, n) for n in which]
+
+    def ends(t, above, below):
+        put(t, 0, 0, activate(t, 0, above) - keep[t, 0])
+        put(t, 3, tiles - 1, keep[t, 1] - activate(t, rows_ext - 1, below))
+
+    def second_norm(t):
+        pair = (acc[t, 0] + term[t, 0], acc[t, 1] - term[t, 3])
+        for r in range(rows):
+            from_tile = slice((r // 2) * width, (r // 2 + 1) * width)
+            n2[r, t * chans : (t + 1) * chans] = norm_silu(pair[r % 2][:, from_tile], half_two[...]).astype(BF)
+
+    def temporal(t):
+        window = jnp.concatenate([n2[r, t * chans : (t + 3) * chans] for r in range(rows)], axis=1)
+        term[t] = dot(wide(wt, 4), window)
+
+    def finish(t):
         for r in range(rows):
             here = slice(r * width, (r + 1) * width)
-            n2[t * chans : (t + 1) * chans, here] = norm_silu(spatial[:, here], half_two[...]).astype(BF)
-
+            o32[t, pl.ds(r, chans, rows), :] = mg[t, r].astype(F32) + term[t][:, here]
+        out_ref[t] = o32[t].astype(BF)
+
+    def weave(first_list, second_list):
+        for n in range(max(len(first_list), len(second_list))):
+            for steps in (first_list, second_list):
+                if n < len(steps):
+                    steps[n]()
+
+    def sides(slot):
+        return (
+            dot_t(ub[slot, jnp.where(first, 1, 0)], pick),
+            dot_t(ub[slot, jnp.where(last, 2, 0)], pick),
+        )
+
+    beside_frames = ((0, 1), (frames_ext - 1, 2))
     own = dot_t(ub[0, 0], pick)
-    for t in range(1, frames_ext - 1):
-        for r in range(1, rows_ext - 1):
-            activate(t, r, own)
+    own_frames = range(1, frames_ext - 1)
+    before = []
+    for t in own_frames:
+        weave(before, rows_in(t, own))
+        before = products(t, 1, 2)
+    weave(before, [])
     arrive_all(edges)
     start_all(beside[1::3])
     start_all(beside[2::3])
     arrive_all(row_halo)
-    above = dot_t(ub[0, jnp.where(first, 1, 0)], pick)
-    below = dot_t(ub[0, jnp.where(last, 2, 0)], pick)
-    for t in range(1, frames_ext - 1):
-        activate(t, 0, above)
-        activate(t, rows_ext - 1, below)
-    for t in range(1, frames_ext - 1):
-        convolve(t)
     for place in range(2, rows):
         arrive_all(frame_halo[place])
-    arrive_all(beside)
+    arrive_all(beside[::3])
+    above, below = sides(0)
+    for t in own_frames:
+        ends(t, above, below)
+    (t_first, slot_first), (t_last, slot_last) = beside_frames
+    rows_first = rows_in(t_first, dot_t(ub[slot_first, 0], pick))
+    rows_last = rows_in(t_last, dot_t(ub[slot_last, 0], pick))
+    heavy = [step for t in own_frames for step in products(t, 0, 3)] + products(t_first, 1, 2)
+    norms = [functools.partial(second_norm, t) for t in own_frames]
+    light = [*rows_first, *(step for n, norm in enumerate(norms) for step in (norm, *rows_last[n : n + 1]))]
+    weave(heavy, [*light, *rows_last[len(norms) :]])
+    arrive_all(beside[1::3])
+    arrive_all(beside[2::3])
     arrive_all(corner_halo)
-    for t, slot in ((0, 1), (frames_ext - 1, 2)):
-        own = dot_t(ub[slot, 0], pick)
-        above = dot_t(ub[slot, jnp.where(first, 1, 0)], pick)
-        below = dot_t(ub[slot, jnp.where(last, 2, 0)], pick)
-        for r in range(rows_ext):
-            activate(t, r, above if r == 0 else below if r == rows_ext - 1 else own)
-        convolve(t)
+    weave(
+        products(t_last, 1, 2),
+        [functools.partial(ends, t, *sides(slot)) for t, slot in beside_frames],
+    )
+    weave(
+        [*products(t_first, 0, 3), *products(t_last, 0, 3), functools.partial(temporal, 0)],
+        [lambda: None, lambda: None, functools.partial(second_norm, t_first)],
+    )
+    second_norm(t_last)
     for t in range(f_dev):
-        temporal = dot(ctt[...], n2[t * chans : (t + 3) * chans, :])
-        for r in range(rows):
-            here = slice(r * width, (r + 1) * width)
-            o32[t, pl.ds(r, chans, rows), :] = mg[t, r].astype(F32) + temporal[:, here]
-        out_ref[t] = o32[t].astype(BF)
-
-    for copies in (row_halo, *frame_halo, corner_halo, edges, beside):
+        if t > 0:
+            temporal(t)
+        finish(t)
+
+    for copies in (gather, scatter, sums, row_halo, *frame_halo, corner_halo, edges, beside):
         sent_all(copies)
+    for copy in across:
+        copy.wait_send()
 
 
 def local(fine, coarse, w_qkv, w_out, w_up, gain_one, conv_space, gain_two, conv_time):
@@ -441,8 +524,7 @@
             pltpu.VMEM((c_dev, chans), BF),
             pltpu.VMEM((3, 3 * chans, chans), BF),
             pltpu.VMEM((3 * chans, chans), BF),
-            pltpu.VMEM((3, chans, 3 * chans), BF),
-            pltpu.VMEM((chans, 3 * chans), BF),
+            pltpu.VMEM((5, pl.cdiv(3 * chans, width), chans, width), BF),
             pltpu.VMEM((f_dev + 2, rows + 2, chans, width), BF),
             pltpu.VMEM((f_dev, rows, chans, width), BF),
             pltpu.VMEM((nf, cells, c_dev), BF),
@@ -451,20 +533,22 @@
             pltpu.VMEM((cf_count, p_dev, chans), BF),
             pltpu.VMEM((group, nf, p_dev, chans), BF),
             pltpu.VMEM((3, 3, span, chans), BF),
-            pltpu.VMEM((f_dev + 2, 3 * chans, (rows + 2) * width), BF),
-            pltpu.VMEM(((f_dev + 2) * chans, rows * width), BF),
+            pltpu.VMEM((f_dev + 2, 4, rows // 2, 3 * chans, width), BF),
+            pltpu.VMEM((rows, (f_dev + 2) * chans, width), BF),
+            pltpu.VMEM((f_dev + 2, 2, chans, width), F32),
+            pltpu.VMEM((f_dev + 2, 2, chans, (rows // 2) * width), F32),
             pltpu.VMEM((chans, width), F32),
             pltpu.VMEM((chans, width), F32),
             pltpu.VMEM((f_dev, chans * rows, width), F32),
             dma((11,)),
             dma((n_halo,)),
             dma((n_halo,)),
-            dma((nf,)),
-            dma((nf,)),
-            dma((nf,)),
-            dma((nf,)),
-            dma((nf, group)),
-            dma((nf, group)),
+            dma((2 * nf,)),
+            dma((2 * nf,)),
+            dma((2 * nf,)),
+            dma((2 * nf,)),
+            dma((2 * nf, group)),
+            dma((2 * nf, group)),
             dma((8,)),
             dma((3, 3)),
         ],

time: 30.7 us -> 27.4 us (0.89)
  Pallas kernels: 29.7 us -> 26.4 us
    pallas_call x1, Pallas kernels: 29.7 us -> 26.4 us  [local(): pl.pallas_call(functools.partial(kernel, nf, nr, cf_count, p_dev, rows),...]
where the time goes in v3:
time: 27.4 us; the launch traced here: 27.3 us
  Pallas kernels  26.4 us (96%)
  local copies, waits for them, and re-layouts  0.84 us (3%)
    pallas_call x1, Pallas kernels, local(): pl.pallas_call(functools.partial(kernel, nf, nr, cf_count, p_dev, rows),...  26.4 us
    unnamed x1, local copies, waits for them, and re-layouts  0.84 us

profile of v3, /device:TPU:1, one launch (start us, length us, event | category | flops | bytes accessed | tf_op | source)
XLA Modules:
  0.0 27.3 jit_solution(6287951111473457109)
XLA Ops:
  0.0 26.4 %decoder_window.1 = bf16[2,1280,128]{2,1,0:T(8,128)(2,1)S(1)} custom-call(bf16[2,1280,128]{2,1,0:T(8,128)(2,1)} %bitcast.10, bf16[32,320]{1,0:T(8,128)(2,1)} %bitcast.11, bf16[3,320,1280]{2,1,0:T(8,128)(2,1)} %bitcast.7, bf16[320,1280]{1,0:T(8,128)(2,1)} %w_out_ref.1, bf16[320,320]{1,0:T(8,128)(2,1)} %w_up_ref.1, f32[320]{0:T(512)} %gain_one_ref.1, ...), custom_call_target="tpu_custom_call" | custom-call | tf_op jit(solution)/shard_map/decoder_window/pallas_call | solution.py:512
  26.4 0.8 %copy.11 = bf16[2,320,4,128]{3,2,1,0:T(4,128)(2,1)} copy(bf16[2,320,4,128]{3,2,1,0:T(4,128)(2,1)S(1)} %bitcast.6) | data formatting | bytes 1310720

commit v4 on v3

--- a/solution.py
+++ b/solution.py
@@ -192,8 +192,6 @@
             n_sem += 1
 
     start_all(frame_halo[0])
-    if rows > 1:
-        start_all(frame_halo[1])
 
     for edge, at in ((me_r == 0, 0), (me_r == nr - 1, rows_ext - 1)):
 
@@ -284,6 +282,8 @@
     )
     start_all(scatter)
     start_all(row_halo)
+    if rows > 1:
+        start_all(frame_halo[1])
     rs_recv[me_f] = rs_send[me_f]
     loads["space1"].wait()
     loads["space2"].wait()
@@ -321,10 +321,6 @@
     up_recv[k_me, me_f] = up_send[coarse_frame(me_f)]
     for place in range(2, rows):
         start_all(frame_halo[place])
-    arrive_all(frame_halo[0])
-    if rows > 1:
-        arrive_all(frame_halo[1])
-    start_all(corner_halo)
     lay(2, ((cs[0].astype(F32) + cs[2].astype(F32) - cs[1].astype(F32)) * 0.5).astype(BF))
     loads["time"].wait()
     lay(4, ct[...])
@@ -367,6 +363,10 @@
             beside.append((copy, there, source) if have is None else (copy, there & have, source & have))
     start_all(edges)
     start_all(beside[::3])
+    arrive_all(frame_halo[0])
+    if rows > 1:
+        arrive_all(frame_halo[1])
+    start_all(corner_halo)
 
     lane_bf = lax.broadcasted_iota(jnp.int32, (chans, width), 1)
     keep_left = jnp.where(lane_bf == 0, 0.0, 1.0).astype(BF)

time: 27.4 us -> 27.3 us (level)
  no operation moved by 1% of the time
where the time goes in v4:
time: 27.3 us; the launch traced here: 27.1 us
  Pallas kernels  26.3 us (96%)
  local copies, waits for them, and re-layouts  0.84 us (3%)
    pallas_call x1, Pallas kernels, local(): pl.pallas_call(functools.partial(kernel, nf, nr, cf_count, p_dev, rows),...  26.3 us
    unnamed x1, local copies, waits for them, and re-layouts  0.84 us

profile of v4, /device:TPU:1, one launch (start us, length us, event | category | flops | bytes accessed | tf_op | source)
XLA Modules:
  0.0 27.1 jit_solution(1844354560316959542)
XLA Ops:
  0.0 26.3 %decoder_window.1 = bf16[2,1280,128]{2,1,0:T(8,128)(2,1)S(1)} custom-call(bf16[2,1280,128]{2,1,0:T(8,128)(2,1)} %bitcast.10, bf16[32,320]{1,0:T(8,128)(2,1)} %bitcast.11, bf16[3,320,1280]{2,1,0:T(8,128)(2,1)} %bitcast.7, bf16[320,1280]{1,0:T(8,128)(2,1)} %w_out_ref.1, bf16[320,320]{1,0:T(8,128)(2,1)} %w_up_ref.1, f32[320]{0:T(512)} %gain_one_ref.1, ...), custom_call_target="tpu_custom_call" | custom-call | tf_op jit(solution)/shard_map/decoder_window/pallas_call | solution.py:512
  26.3 0.8 %copy.11 = bf16[2,320,4,128]{3,2,1,0:T(4,128)(2,1)} copy(bf16[2,320,4,128]{3,2,1,0:T(4,128)(2,1)S(1)} %bitcast.6) | data formatting | bytes 1310720
